TPU v7x, 32 devices: a whole 2x2x4 slice. The times are simulated.
32 devices in a mesh: batch: 2 (over x), row: 4 (over z), col: 4 (over y, core).
Axes of the slice: x: 2, y: 2, z: 4, core: 2. Of those that a mesh axis runs over, the one named last changes fastest.
Arguments:
- l_mat: bfloat16 [16384, 8192], P(('batch', 'row'), 'col'), parts along dimension 0
- b_mat: bfloat16 [16384, 16384], P(('batch', 'row'), 'col'), parts along dimension 0
Outputs:
- output: bfloat16 [16384, 16384], P(('batch', 'row'), 'col'), parts along dimension 0
There are 2 independent parts. A program takes and returns all parts, laid end to end along the dimension named above; each array names one.
All inputs are finite; a program needn't handle non-finite values.
Results may differ from a plain program's by a relative error of at most 0.001.
Values are sent between devices in bfloat16 or wider.
A program may use at most 1 GiB of HBM per device.

v0:
```python
import jax
import jax.numpy as jnp
from jax import lax
from jax.sharding import PartitionSpec as P


def solution(mesh):
    block_spec = P(('batch', 'row'), 'col')

    def local_product(l_block, b_block):
        l_strip = lax.all_gather(l_block, 'col', axis=1, tiled=True)
        b_strip = lax.all_gather(b_block, 'row', axis=0, tiled=True)
        result = jnp.dot(l_strip, b_strip, preferred_element_type=jnp.float32)
        return result.astype(b_block.dtype)

    return jax.shard_map(local_product, mesh=mesh, in_specs=(block_spec, block_spec), out_specs=block_spec, check_vma=False)
```

profile of v0, /device:TPU:24, one launch (start us, length us, event | category | flops | bytes accessed | tf_op | source)
XLA Modules:
  0.0 1481.8 jit_solution(14189205302922720124)
XLA Ops:
  6.5 0.0 all-gather.3.cloned.1.call-start
  6.5 0.7 all-gather.3.cloned.1.call-update
  7.3 0.0 all-gather.5.cloned.1.call-start
  7.3 0.7 all-gather.5.cloned.1.call-update
  8.0 204.0 %all-gather.3.cloned.1.call-done = bf16[2048,8192]{1,0:T(8,128)(2,1)} async-done(((bf16[2048,2048]{1,0:T(8,128)(2,1)}), bf16[2048,8192]{1,0:T(8,128)(2,1)}) %all-gather.3.cloned.1.call-update) | async-done | bytes 33554448 | tf_op jit(solution)/shard_map/all_gather | solution.py:11
  212.0 1110.3 %all-gather.5.cloned.1.call-done = bf16[8192,4096]{1,0:T(8,128)(2,1)} async-done(((bf16[2048,4096]{1,0:T(8,128)(2,1)}), bf16[8192,4096]{1,0:T(8,128)(2,1)}) %all-gather.5.cloned.1.call-update) | async-done | bytes 67108880 | tf_op jit(solution)/shard_map/all_gather | solution.py:12
  1322.4 152.6 %convolution_convert_fusion = bf16[2048,4096]{1,0:T(8,128)(2,1)} fusion(bf16[2048,8192]{1,0:T(8,128)(2,1)} %all-gather.3.cloned.1.call-done, bf16[8192,4096]{1,0:T(8,128)(2,1)} %all-gather.5.cloned.1.call-done), kind=kOutput, calls=%fused_computation | convolution fusion | flops 137447342080 | bytes 117440512 | tf_op jit(solution)/shard_map/dot_general | solution.py:13
Async XLA Ops:
  6.5 205.5 %all-gather.3.cloned.1.call-start = ((), (), s32[]{:S(2)}) async-start(), calls=%async_computation | async-start | bytes 41943040 | tf_op jit(solution)/shard_map/all_gather | solution.py:11
  7.3 1315.1 %all-gather.5.cloned.1.call-start = ((), (), s32[]{:S(2)}) async-start(), calls=%async_computation.1 | async-start | bytes 83886080 | tf_op jit(solution)/shard_map/all_gather | solution.py:12
Sparse Core Ops, SparseCore 0:
  8.9 203.1 all-gather.2
  213.6 1108.6 all-gather.4
where the time goes:
time: 1490 us; the launch traced here: 1480 us
  waiting for transfers between devices  1320 us (89%)
  matrix products  153 us (10%)
    all_gather x1, waiting for transfers between devices, local_product(): b_strip = lax.all_gather(b_block, 'row', axis=0, tiled=True)  1110 us
    all_gather x1, waiting for transfers between devices, local_product(): l_strip = lax.all_gather(l_block, 'col', axis=1, tiled=True)  204 us
    dot_general x1, matrix products, local_product(): result = jnp.dot(l_strip, b_strip, preferred_element_type=jnp.float32)  153 us
  transfers between devices with their start and end apart: 2, of which 2 were waited for; matrix products, arithmetic and copies ran while one was open for 0% of the time, Pallas kernels for 0%

commit v1 on v0

v1 whole, which is shorter than its diff:
```python
import functools

import jax
import jax.numpy as jnp
from jax import lax
from jax.experimental import pallas as pl
from jax.experimental.pallas import tpu as pltpu
from jax.sharding import PartitionSpec as P

MESH = pl.DeviceIdType.MESH
TILES = 4
CHUNK = 256


def mid_order(chunks):
    return [(1, c) for c in range(chunks)] + [(0, c) for c in range(chunks)]


def kernel(
    l_ref, b_ref, x_ref, rb_ref, lg_ref,
    l3_v, b_v, strip_v, x3_v, xo_v,
    b0_rx, b1_rx, b3_rx, l_rx, l3_rx, cross_rx, x3_rx,
    b_tx, fwd_tx, l_tx, l3_tx, x3_tx,
    load_sem, strip_sem, out_sem, l3_sem,
):
    n, m = b_ref.shape
    half = n // 2
    rt = n // TILES
    w = CHUNK
    chunks = m // w
    batch, row, col = (lax.axis_index(a) for a in ("batch", "row", "col"))
    core_peer = col + 1 - 2 * lax.rem(col, 2)
    y_peer = lax.rem(col + 2, 4)
    far = lax.rem(core_peer + 2, 4)

    def remote(src, dst, send, recv, r, c):
        return pltpu.make_async_remote_copy(
            src_ref=src, dst_ref=dst, send_sem=send, recv_sem=recv,
            device_id=(batch, r, c), device_id_type=MESH,
        )

    def arrived(dst, sem):
        pltpu.make_async_copy(dst, dst, sem).wait()

    def own_chunk(c):
        return b_ref.at[:, pl.ds(pl.multiple_of(c * w, w), w)]

    def x_tile(i, c):
        return x_ref.at[pl.ds(i * rt, rt), pl.ds(pl.multiple_of(c * w, w), w)]

    def l_exchange_start():
        remote(l_ref, lg_ref.at[0, col], l_tx.at[0], l_rx.at[0], row, y_peer).start()
        remote(l_ref, lg_ref.at[0, col], l_tx.at[1], l_rx.at[1], row, core_peer).start()

    def l_forward():
        blk = lg_ref.at[0, y_peer]
        arrived(blk, l_rx.at[0])
        remote(blk, blk, l_tx.at[2], l_rx.at[2], row, core_peer).start()

    def l_exchange_end():
        arrived(lg_ref.at[0, core_peer], l_rx.at[1])
        arrived(lg_ref.at[0, far], l_rx.at[2])

    def l_exchange_drain():
        for s in range(3):
            arrived(l_ref, l_tx.at[s])

    def strip_parts(r, i):
        return [(k, n if k < r else (i + 1) * rt) for k in range(r + 1)]

    def strip_start(r, i):
        for k, depth in strip_parts(r, i):
            dst = strip_v.at[i % 2, :, pl.ds(k * n, depth)]
            rows = pl.ds(i * rt, rt)

            @pl.when(col == k)
            def _(dst=dst, rows=rows, depth=depth):
                pltpu.make_async_copy(l_ref.at[rows, pl.ds(0, depth)], dst, strip_sem.at[i % 2]).start()

            @pl.when(col != k)
            def _(dst=dst, rows=rows, depth=depth, k=k):
                pltpu.make_async_copy(lg_ref.at[0, k, rows, pl.ds(0, depth)], dst, strip_sem.at[i % 2]).start()

    def strip_wait(r, i):
        depth = r * n + (i + 1) * rt
        ref = strip_v.at[i % 2, :, pl.ds(0, depth)]
        pltpu.make_async_copy(ref, ref, strip_sem.at[i % 2]).wait()

    def load(c, slot, k, src):
        return pltpu.make_async_copy(src, b_v.at[slot, pl.ds(k * n, n), :], load_sem.at[slot, k])

    def own_rows(r, c, slot):
        for i in range(TILES):
            strip_wait(r, i)
            if i + 1 < TILES:
                strip_start(r, i + 1)
            else:
                @pl.when(c + 1 < chunks)
                def _():
                    strip_start(r, 0)
            depth = r * n + (i + 1) * rt
            acc = jnp.dot(
                strip_v[i % 2, :, :depth], b_v[slot, :depth, :], preferred_element_type=jnp.float32
            )
            out = pltpu.make_async_copy(xo_v.at[i % 2], x_tile(i, c), out_sem.at[i % 2])
            if i >= 2:
                out.wait()
            else:
                @pl.when(c > 0)
                def _(out=out):
                    out.wait()
            xo_v[i % 2] = acc.astype(xo_v.dtype)
            out.start()

    def own_rows_drain():
        for s in range(2):
            pltpu.make_async_copy(xo_v.at[s], x_tile(s, 0), out_sem.at[s]).wait()

    def simple_rows(r, prior):
        def loads(c, slot):
            return [load(c, slot, k, ref(c)) for k, ref in prior]

        for cp in loads(0, 0):
            cp.start()
        strip_start(r, 0)

        def step(c, carry):
            slot = lax.rem(c, 2)
            for cp in loads(c, slot):
                cp.wait()

            @pl.when(c + 1 < chunks)
            def _():
                for cp in loads(c + 1, 1 - slot):
                    cp.start()

            own_rows(r, c, slot)
            return carry

        lax.fori_loop(0, chunks, step, 0)
        own_rows_drain()

    @pl.when(row == 0)
    def _():
        def send(c, carry):
            remote(own_chunk(c), rb_ref.at[0, c], b_tx, b0_rx.at[c], 1, col).start()
            return carry

        lax.fori_loop(0, chunks, send, 0)
        l_exchange_start()
        l_forward()
        l_exchange_end()
        simple_rows(0, [(0, own_chunk)])
        l_exchange_drain()
        arrived(b_ref, b_tx)

    @pl.when(row == 1)
    def _():
        l_exchange_start()

        def send_own(c, carry):
            remote(own_chunk(c), rb_ref.at[1, c], b_tx, b1_rx.at[c], 2, col).start()
            return carry

        def forward(c, carry):
            blk = rb_ref.at[0, c]
            arrived(blk, b0_rx.at[c])
            remote(blk, blk, fwd_tx, b0_rx.at[c], 2, col).start()
            return carry

        lax.fori_loop(0, chunks, send_own, 0)
        lax.fori_loop(0, chunks, forward, 0)
        l_forward()
        l_exchange_end()
        simple_rows(1, [(0, lambda c: rb_ref.at[0, c]), (1, own_chunk)])
        l_exchange_drain()
        arrived(b_ref, b_tx)
        arrived(rb_ref.at[0], fwd_tx)

    @pl.when(row == 2)
    def _():
        l_exchange_start()
        lo, hi = pl.ds(0, half), pl.ds(half, half)

        def own(p):
            return lg_ref.at[1, col, p]

        def other(p):
            return lg_ref.at[1, y_peer, p]

        arrived(own(lo), l3_rx.at[0])
        remote(own(lo), own(lo), l3_tx.at[0], l3_rx.at[2], row, y_peer).start()
        remote(own(lo), own(lo), l3_tx.at[1], l3_rx.at[4], row, core_peer).start()
        arrived(own(hi), l3_rx.at[1])
        remote(own(hi), own(hi), l3_tx.at[2], l3_rx.at[5], row, core_peer).start()
        l_forward()
        arrived(other(lo), l3_rx.at[2])
        remote(other(lo), other(lo), l3_tx.at[3], l3_rx.at[6], row, core_peer).start()
        arrived(other(hi), l3_rx.at[3])
        remote(other(hi), other(hi), l3_tx.at[4], l3_rx.at[7], row, core_peer).start()
        l_exchange_end()
        for s, (blk, p) in enumerate(((core_peer, lo), (core_peer, hi), (far, lo), (far, hi))):
            arrived(lg_ref.at[1, blk, p], l3_rx.at[4 + s])
        for k in range(4):
            pltpu.make_async_copy(lg_ref.at[1, k], l3_v.at[:, pl.ds(k * n, n)], l3_sem).start()

        def early(c, slot):
            return [
                load(c, slot, 1, rb_ref.at[1, c]), load(c, slot, 2, own_chunk(c)), load(c, slot, 3, rb_ref.at[2, c])
            ]

        def prefetch(c, slot):
            arrived(rb_ref.at[1, c], b1_rx.at[c])
            arrived(rb_ref.at[2, c], b3_rx.at[c])
            for cp in early(c, slot):
                cp.start()

        def x3_send(i, c, slot):
            return remote(x3_v.at[slot, i], x_tile(i, c), x3_tx.at[slot, i], x3_rx, 3, col)

        prefetch(0, 0)
        strip_start(2, 0)
        pltpu.make_async_copy(l3_v, l3_v, l3_sem).wait()

        def step(c, carry):
            slot = lax.rem(c, 2)
            arrived(rb_ref.at[0, c], b0_rx.at[c])
            last = load(c, slot, 0, rb_ref.at[0, c])
            last.start()
            for cp in early(c, slot):
                cp.wait()
            last.wait()
            for i in range(TILES):
                @pl.when(c >= 2)
                def _(i=i):
                    x3_send(i, c, slot).wait_send()

                depth = 3 * n + (i + 1) * rt
                acc = jnp.dot(
                    l3_v[pl.ds(i * rt, rt), :depth], b_v[slot, :depth, :], preferred_element_type=jnp.float32
                )
                x3_v[slot, i] = acc.astype(x3_v.dtype)
                if i:
                    x3_send(i - 1, c, slot).start()

            @pl.when(c + 1 < chunks)
            def _():
                prefetch(c + 1, 1 - slot)

            x3_send(TILES - 1, c, slot).start()
            own_rows(2, c, slot)
            return carry

        lax.fori_loop(0, chunks, step, 0)
        own_rows_drain()
        for slot in range(2):
            for i in range(TILES):
                x3_send(i, 0, slot).wait_send()
        l_exchange_drain()
        for s in range(5):
            arrived(own(lo), l3_tx.at[s])

    @pl.when(row == 3)
    def _():
        lo, hi = pl.ds(0, half), pl.ds(half, half)
        for s, p in enumerate((lo, hi)):
            remote(l_ref.at[p], lg_ref.at[1, col, p], l3_tx.at[s], l3_rx.at[s], 2, col).start()
        remote(l_ref.at[hi], lg_ref.at[1, col, hi], l3_tx.at[2], cross_rx, row, y_peer).start()
        blk = lg_ref.at[1, y_peer, hi]
        arrived(blk, cross_rx)
        remote(blk, blk, l3_tx.at[3], l3_rx.at[3], 2, col).start()

        def send(c, carry):
            remote(own_chunk(c), rb_ref.at[2, c], b_tx, b3_rx.at[c], 2, col).start()
            return carry

        lax.fori_loop(0, chunks, send, 0)
        for s in range(4):
            arrived(blk, l3_tx.at[s])
        arrived(b_ref, b_tx)
        arrived(x_ref, x3_rx)


def solution(mesh):
    block_spec = P(("batch", "row"), "col")

    def local_product(l_block, b_block):
        n, m = b_block.shape
        rt = n // TILES
        chunks = m // CHUNK
        dma = pltpu.SemaphoreType.DMA
        hbm = pl.BlockSpec(memory_space=pl.ANY)
        x, _, _ = pl.pallas_call(
            kernel,
            out_shape=(
                jax.ShapeDtypeStruct((n, m), b_block.dtype),
                jax.ShapeDtypeStruct((3, chunks, n, CHUNK), b_block.dtype),
                jax.ShapeDtypeStruct((2, 4, n, n), l_block.dtype),
            ),
            in_specs=[hbm, hbm],
            out_specs=(hbm, hbm, hbm),
            scratch_shapes=[
                pltpu.VMEM((n, 4 * n), l_block.dtype),
                pltpu.VMEM((2, 4 * n, CHUNK), b_block.dtype),
                pltpu.VMEM((2, rt, 3 * n), l_block.dtype),
                pltpu.VMEM((2, TILES, rt, CHUNK), b_block.dtype),
                pltpu.VMEM((2, rt, CHUNK), b_block.dtype),
                dma((chunks,)), dma((chunks,)), dma((chunks,)), dma((3,)), dma((8,)), dma, dma,
                dma, dma, dma((3,)), dma((5,)), dma((2, TILES)),
                dma((2, 4)), dma((2,)), dma((2,)), dma,
            ],
            compiler_params=pltpu.CompilerParams(has_side_effects=True, vmem_limit_bytes=66 * 1000 * 1000),
        )(l_block, b_block)
        return x

    return jax.shard_map(
        local_product, mesh=mesh, in_specs=(block_spec, block_spec), out_specs=block_spec, check_vma=False
    )
```

time: 1490 us -> 886 us (0.59)
  waiting for transfers between devices: 1320 us -> 0 us
  Pallas kernels: 0 us -> 870 us
  matrix products: 153 us -> 0 us
    all_gather x2 -> x0, waiting for transfers between devices: 1310 us -> none  [the longest x1 1110 us: local_product(): b_strip = lax.all_gather(b_block, 'row', axis=0, tiled=True)]
    pallas_call x0 -> x1, Pallas kernels: none -> 870 us  [local_product(): pl.pallas_call(kernel, out_shape=(jax.ShapeDtypeStruct((n, m), b_block.dt...]
    dot_general x1 -> x0, matrix products: 153 us -> none  [local_product(): result = jnp.dot(l_strip, b_strip, preferred_element_type=jnp.float32)]
  transfers between devices with their start and end apart: 2 -> 0, of which waited for: 2 -> 0; matrix products, arithmetic and copies ran while one was open for 0% -> 0% of each run, Pallas kernels for 0% -> 0%
where the time goes in v1:
time: 886 us; the launch traced here: 884 us
  Pallas kernels  870 us (98%)
  local copies, waits for them, and re-layouts  14.1 us (2%)
    pallas_call x1, Pallas kernels, local_product(): pl.pallas_call(kernel, out_shape=(jax.ShapeDtypeStruct((n, m), b_block.dt...  870 us

profile of v1, /device:TPU:24, one launch (start us, length us, event | category | flops | bytes accessed | tf_op | source)
XLA Modules:
  0.0 883.9 jit_solution(10138747007049009260)
XLA Ops:
  0.0 869.9 %shard_map.28 = (bf16[2048,4096]{1,0:T(8,128)(2,1)}, bf16[3,16,2048,256]{3,2,1,0:T(8,128)(2,1)}, bf16[2,4,2048,2048]{3,2,1,0:T(8,128)(2,1)}) custom-call(bf16[2048,2048]{1,0:T(8,128)(2,1)} %l_ref.1, bf16[2048,4096]{1,0:T(8,128)(2,1)} %b_ref.1), custom_call_target="tpu_custom_call" | custom-call | tf_op jit(solution)/shard_map/pallas_call | solution.py:293
  869.9 14.1 %copy.4 = bf16[2048,4096]{1,0:T(8,128)(2,1)} copy(bf16[2048,4096]{1,0:T(8,128)(2,1)} %get-tuple-element.6) | data formatting | bytes 33554432

commit v2 on v1

--- a/solution.py
+++ b/solution.py
@@ -46,7 +46,7 @@
         return b_ref.at[:, pl.ds(pl.multiple_of(c * w, w), w)]
 
     def x_tile(i, c):
-        return x_ref.at[pl.ds(i * rt, rt), pl.ds(pl.multiple_of(c * w, w), w)]
+        return x_ref.at[pl.ds(pl.multiple_of(i * rt, rt), rt), pl.ds(pl.multiple_of(c * w, w), w)]
 
     def l_exchange_start():
         remote(l_ref, lg_ref.at[0, col], l_tx.at[0], l_rx.at[0], row, y_peer).start()
@@ -65,52 +65,52 @@
         for s in range(3):
             arrived(l_ref, l_tx.at[s])
 
-    def strip_parts(r, i):
-        return [(k, n if k < r else (i + 1) * rt) for k in range(r + 1)]
-
     def strip_start(r, i):
-        for k, depth in strip_parts(r, i):
-            dst = strip_v.at[i % 2, :, pl.ds(k * n, depth)]
-            rows = pl.ds(i * rt, rt)
+        slot = lax.rem(i, 2)
+        rows = pl.ds(pl.multiple_of(i * rt, rt), rt)
+        for k in range(r + 1):
+            dst = strip_v.at[slot, :, pl.ds(k * n, n)]
 
             @pl.when(col == k)
-            def _(dst=dst, rows=rows, depth=depth):
-                pltpu.make_async_copy(l_ref.at[rows, pl.ds(0, depth)], dst, strip_sem.at[i % 2]).start()
+            def _(dst=dst):
+                pltpu.make_async_copy(l_ref.at[rows], dst, strip_sem.at[slot]).start()
 
             @pl.when(col != k)
-            def _(dst=dst, rows=rows, depth=depth, k=k):
-                pltpu.make_async_copy(lg_ref.at[0, k, rows, pl.ds(0, depth)], dst, strip_sem.at[i % 2]).start()
+            def _(dst=dst, k=k):
+                pltpu.make_async_copy(lg_ref.at[0, k, rows], dst, strip_sem.at[slot]).start()
 
     def strip_wait(r, i):
-        depth = r * n + (i + 1) * rt
-        ref = strip_v.at[i % 2, :, pl.ds(0, depth)]
-        pltpu.make_async_copy(ref, ref, strip_sem.at[i % 2]).wait()
+        slot = lax.rem(i, 2)
+        ref = strip_v.at[slot, :, pl.ds(0, (r + 1) * n)]
+        pltpu.make_async_copy(ref, ref, strip_sem.at[slot]).wait()
 
     def load(c, slot, k, src):
         return pltpu.make_async_copy(src, b_v.at[slot, pl.ds(k * n, n), :], load_sem.at[slot, k])
 
     def own_rows(r, c, slot):
-        for i in range(TILES):
+        depth = (r + 1) * n
+
+        def tile(i, carry):
+            part = lax.rem(i, 2)
             strip_wait(r, i)
-            if i + 1 < TILES:
-                strip_start(r, i + 1)
-            else:
-                @pl.when(c + 1 < chunks)
-                def _():
-                    strip_start(r, 0)
-            depth = r * n + (i + 1) * rt
-            acc = jnp.dot(
-                strip_v[i % 2, :, :depth], b_v[slot, :depth, :], preferred_element_type=jnp.float32
-            )
-            out = pltpu.make_async_copy(xo_v.at[i % 2], x_tile(i, c), out_sem.at[i % 2])
-            if i >= 2:
+
+            @pl.when((i + 1 < TILES) | (c + 1 < chunks))
+            def _():
+                strip_start(r, lax.rem(i + 1, TILES))
+
+            out = pltpu.make_async_copy(xo_v.at[part], x_tile(i, c), out_sem.at[part])
+
+            @pl.when((i >= 2) | (c > 0))
+            def _():
                 out.wait()
-            else:
-                @pl.when(c > 0)
-                def _(out=out):
-                    out.wait()
-            xo_v[i % 2] = acc.astype(xo_v.dtype)
+
+            xo_v[part] = jnp.dot(
+                strip_v[part, :, :depth], b_v[slot, :depth, :], preferred_element_type=jnp.float32
+            ).astype(xo_v.dtype)
             out.start()
+            return carry
+
+        lax.fori_loop(0, TILES, tile, 0)
 
     def own_rows_drain():
         for s in range(2):
@@ -230,18 +230,23 @@
             for cp in early(c, slot):
                 cp.wait()
             last.wait()
-            for i in range(TILES):
+            def tile(i, inner):
                 @pl.when(c >= 2)
-                def _(i=i):
+                def _():
                     x3_send(i, c, slot).wait_send()
 
-                depth = 3 * n + (i + 1) * rt
-                acc = jnp.dot(
-                    l3_v[pl.ds(i * rt, rt), :depth], b_v[slot, :depth, :], preferred_element_type=jnp.float32
-                )
-                x3_v[slot, i] = acc.astype(x3_v.dtype)
-                if i:
+                rows = pl.ds(pl.multiple_of(i * rt, rt), rt)
+                x3_v[slot, i] = jnp.dot(
+                    l3_v[rows, :], b_v[slot], preferred_element_type=jnp.float32
+                ).astype(x3_v.dtype)
+
+                @pl.when(i > 0)
+                def _():
                     x3_send(i - 1, c, slot).start()
+
+                return inner
+
+            lax.fori_loop(0, TILES, tile, 0)
 
             @pl.when(c + 1 < chunks)
             def _():

time: 886 us -> 774 us (0.87)
  Pallas kernels: 870 us -> 758 us
    pallas_call x1, Pallas kernels: 870 us -> 758 us  [local_product(): pl.pallas_call(kernel, out_shape=(jax.ShapeDtypeStruct((n, m), b_block.dt...]
where the time goes in v2:
time: 774 us; the launch traced here: 772 us
  Pallas kernels  758 us (98%)
  local copies, waits for them, and re-layouts  14.1 us (2%)
    pallas_call x1, Pallas kernels, local_product(): pl.pallas_call(kernel, out_shape=(jax.ShapeDtypeStruct((n, m), b_block.dt...  758 us

profile of v2, /device:TPU:24, one launch (start us, length us, event | category | flops | bytes accessed | tf_op | source)
XLA Modules:
  0.0 772.1 jit_solution(16621188797400897469)
XLA Ops:
  0.0 758.0 %shard_map.28 = (bf16[2048,4096]{1,0:T(8,128)(2,1)}, bf16[3,16,2048,256]{3,2,1,0:T(8,128)(2,1)}, bf16[2,4,2048,2048]{3,2,1,0:T(8,128)(2,1)}) custom-call(bf16[2048,2048]{1,0:T(8,128)(2,1)} %l_ref.1, bf16[2048,4096]{1,0:T(8,128)(2,1)} %b_ref.1), custom_call_target="tpu_custom_call" | custom-call | tf_op jit(solution)/shard_map/pallas_call | solution.py:298
  758.0 14.1 %copy.4 = bf16[2048,4096]{1,0:T(8,128)(2,1)} copy(bf16[2048,4096]{1,0:T(8,128)(2,1)} %get-tuple-element.6) | data formatting | bytes 33554432

commit v3 on v2

--- a/solution.py
+++ b/solution.py
@@ -13,21 +13,31 @@
 
 
 def mid_order(chunks):
-    return [(1, c) for c in range(chunks)] + [(0, c) for c in range(chunks)]
+    first = chunks * 3 // 4
+    late = list(range(first, chunks - 2))
+    gap = -(-(chunks - 2) // (len(late) + 1))
+    order = [(1, c) for c in range(first)]
+    for c in range(chunks - 2):
+        order.append((0, c))
+        if late and (c + 1) % gap == 0:
+            order.append((1, late.pop(0)))
+    assert not late
+    return order + [(k, c) for c in (chunks - 2, chunks - 1) for k in (1, 0)]
 
 
 def kernel(
     l_ref, b_ref, x_ref, rb_ref, lg_ref,
-    l3_v, b_v, strip_v, x3_v, xo_v,
+    l3_v, b_v, strip_v, x3_v, xo_v, p3_v, p2_v,
     b0_rx, b1_rx, b3_rx, l_rx, l3_rx, cross_rx, x3_rx,
     b_tx, fwd_tx, l_tx, l3_tx, x3_tx,
-    load_sem, strip_sem, out_sem, l3_sem,
+    load_sem, strip_sem, out_sem, l3_sem, piece_sem,
 ):
     n, m = b_ref.shape
     half = n // 2
     rt = n // TILES
     w = CHUNK
     chunks = m // w
+    edge, hw = chunks - 1, w // 2
     batch, row, col = (lax.axis_index(a) for a in ("batch", "row", "col"))
     core_peer = col + 1 - 2 * lax.rem(col, 2)
     y_peer = lax.rem(col + 2, 4)
@@ -87,14 +97,14 @@
     def load(c, slot, k, src):
         return pltpu.make_async_copy(src, b_v.at[slot, pl.ds(k * n, n), :], load_sem.at[slot, k])
 
-    def own_rows(r, c, slot):
+    def own_rows(r, c, slot, end):
         depth = (r + 1) * n
 
         def tile(i, carry):
             part = lax.rem(i, 2)
             strip_wait(r, i)
 
-            @pl.when((i + 1 < TILES) | (c + 1 < chunks))
+            @pl.when((i + 1 < TILES) | (c + 1 < end))
             def _():
                 strip_start(r, lax.rem(i + 1, TILES))
 
@@ -134,7 +144,7 @@
                 for cp in loads(c + 1, 1 - slot):
                     cp.start()
 
-            own_rows(r, c, slot)
+            own_rows(r, c, slot, chunks)
             return carry
 
         lax.fori_loop(0, chunks, step, 0)
@@ -158,18 +168,18 @@
     def _():
         l_exchange_start()
 
-        def send_own(c, carry):
-            remote(own_chunk(c), rb_ref.at[1, c], b_tx, b1_rx.at[c], 2, col).start()
-            return carry
-
-        def forward(c, carry):
-            blk = rb_ref.at[0, c]
+        for k, c in mid_order(chunks):
+            blk = rb_ref.at[k, c]
+            if k == 1:
+                remote(own_chunk(c), blk, b_tx, b1_rx.at[c], 2, col).start()
+                continue
             arrived(blk, b0_rx.at[c])
-            remote(blk, blk, fwd_tx, b0_rx.at[c], 2, col).start()
-            return carry
-
-        lax.fori_loop(0, chunks, send_own, 0)
-        lax.fori_loop(0, chunks, forward, 0)
+            if c < edge:
+                remote(blk, blk, fwd_tx, b0_rx.at[c], 2, col).start()
+                continue
+            for h in range(2):
+                part = blk.at[:, pl.ds(h * hw, hw)]
+                remote(part, part, fwd_tx, b0_rx.at[c + h], 2, col).start()
         l_forward()
         l_exchange_end()
         simple_rows(1, [(0, lambda c: rb_ref.at[0, c]), (1, own_chunk)])
@@ -204,32 +214,82 @@
         for k in range(4):
             pltpu.make_async_copy(lg_ref.at[1, k], l3_v.at[:, pl.ds(k * n, n)], l3_sem).start()
 
-        def early(c, slot):
-            return [
-                load(c, slot, 1, rb_ref.at[1, c]), load(c, slot, 2, own_chunk(c)), load(c, slot, 3, rb_ref.at[2, c])
-            ]
-
-        def prefetch(c, slot):
+        def load1(c, slot):
+            return load(c, slot, 1, rb_ref.at[1, c])
+
+        def load23(c, slot):
+            return load(c, slot, 2, own_chunk(c)), load(c, slot, 3, rb_ref.at[2, c])
+
+        def prefetch23(c, slot):
+            arrived(rb_ref.at[2, c], b3_rx.at[c])
+            for cp in load23(c, slot):
+                cp.start()
+
+        def prefetch1(c, slot):
             arrived(rb_ref.at[1, c], b1_rx.at[c])
-            arrived(rb_ref.at[2, c], b3_rx.at[c])
-            for cp in early(c, slot):
-                cp.start()
+            load1(c, slot).start()
 
         def x3_send(i, c, slot):
             return remote(x3_v.at[slot, i], x_tile(i, c), x3_tx.at[slot, i], x3_rx, 3, col)
 
-        prefetch(0, 0)
+        prefetch23(0, 0)
+        prefetch1(0, 0)
         strip_start(2, 0)
         pltpu.make_async_copy(l3_v, l3_v, l3_sem).wait()
 
+        e_slot, e_spare = edge % 2, 1 - edge % 2
+
+        def piece(s):
+            q = lax.rem(s, 6)
+            return strip_v.at[q // 3, :, pl.ds(pl.multiple_of(lax.rem(q, 3) * n, n), n)]
+
+        def piece_start(s):
+            k, i = 2 - s // TILES, s % TILES
+            rows = pl.ds(i * rt, rt)
+
+            @pl.when(col == k)
+            def _():
+                pltpu.make_async_copy(l_ref.at[rows], piece(s), piece_sem.at[s]).start()
+
+            @pl.when(col != k)
+            def _():
+                pltpu.make_async_copy(lg_ref.at[0, k, rows], piece(s), piece_sem.at[s]).start()
+
+        def piece_wait(s):
+            arrived(piece(s), piece_sem.at[s])
+
+        def tile_rows(i):
+            return pl.ds(pl.multiple_of(i * rt, rt), rt)
+
+        def dot(a, b):
+            return jnp.dot(a, b, preferred_element_type=jnp.float32)
+
+        def terms23():
+            for s in range(TILES):
+                piece_start(s)
+            prefetch23(edge, e_slot)
+            for cp in load23(edge, e_slot):
+                cp.wait()
+
+            def tile(i, carry):
+                rows = tile_rows(i)
+                p3_v[rows, :] = dot(l3_v[rows, 2 * n :], b_v[e_slot, 2 * n :, :])
+                piece_wait(i)
+                p2_v[rows, :] = dot(piece(i)[...], b_v[e_slot, 2 * n : 3 * n, :])
+                return carry
+
+            lax.fori_loop(0, TILES, tile, 0)
+            prefetch1(edge - 1, e_spare)
+            strip_start(2, 0)
+
         def step(c, carry):
             slot = lax.rem(c, 2)
+            pl.when(c == edge - 1)(terms23)
             arrived(rb_ref.at[0, c], b0_rx.at[c])
             last = load(c, slot, 0, rb_ref.at[0, c])
             last.start()
-            for cp in early(c, slot):
+            for cp in (load1(c, slot), *load23(c, slot), last):
                 cp.wait()
-            last.wait()
             def tile(i, inner):
                 @pl.when(c >= 2)
                 def _():
@@ -248,19 +308,105 @@
 
             lax.fori_loop(0, TILES, tile, 0)
 
-            @pl.when(c + 1 < chunks)
-            def _():
-                prefetch(c + 1, 1 - slot)
-
             x3_send(TILES - 1, c, slot).start()
-            own_rows(2, c, slot)
-            return carry
-
-        lax.fori_loop(0, chunks, step, 0)
+
+            @pl.when(c + 1 < edge)
+            def _():
+                prefetch23(c + 1, 1 - slot)
+
+            @pl.when(c + 2 < edge)
+            def _():
+                prefetch1(c + 1, 1 - slot)
+
+            own_rows(2, c, slot, edge - 1)
+            return carry
+
+        lax.fori_loop(0, edge, step, 0)
         own_rows_drain()
-        for slot in range(2):
+
+        for s in range(TILES, TILES + 6):
+            piece_start(s)
+        prefetch1(edge, e_slot)
+        load1(edge, e_slot).wait()
+
+        def terms1(i, carry):
+            rows = tile_rows(i)
+            p3_v[rows, :] += dot(l3_v[rows, n : 2 * n], b_v[e_slot, n : 2 * n, :])
+            piece_wait(TILES + i)
+            p2_v[rows, :] += dot(piece(TILES + i)[...], b_v[e_slot, n : 2 * n, :])
+            return carry
+
+        lax.fori_loop(0, TILES, terms1, 0)
+        for s in range(10, 12):
+            piece_start(s)
+        for s in range(2):
             for i in range(TILES):
-                x3_send(i, 0, slot).wait_send()
+                x3_send(i, 0, s).wait_send()
+
+        def half_lanes(h):
+            return pl.ds(pl.multiple_of(h * hw, hw), hw)
+
+        def half_tile(i, h):
+            return x_ref.at[tile_rows(i), pl.ds(pl.multiple_of(edge * w + h * hw, hw), hw)]
+
+        def x3_half(i, h):
+            return remote(
+                x3_v.at[e_slot, i, :, half_lanes(h)], half_tile(i, h), x3_tx.at[e_slot, i], x3_rx, 3, col
+            )
+
+        def x2_half(i, h):
+            return pltpu.make_async_copy(
+                x3_v.at[e_spare, i, :, half_lanes(h)], half_tile(i, h), x3_tx.at[e_spare, i]
+            )
+
+        def half_step(h, carry):
+            lanes = half_lanes(h)
+            part = rb_ref.at[0, edge, :, lanes]
+            arrived(part, b0_rx.at[edge + h])
+            last = pltpu.make_async_copy(part, b_v.at[e_slot, pl.ds(0, n), lanes], load_sem.at[e_slot, 0])
+            last.start()
+            last.wait()
+
+            def tile3(i, inner):
+                rows = tile_rows(i)
+                x3_v[e_slot, i, :, lanes] = (
+                    p3_v[rows, lanes] + dot(l3_v[rows, :n], b_v[e_slot, :n, lanes])
+                ).astype(x3_v.dtype)
+
+                @pl.when(i > 0)
+                def _():
+                    x3_half(i - 1, h).start()
+
+                return inner
+
+            def tile2(i, inner):
+                @pl.when(h == 0)
+                def _():
+                    piece_wait(2 * TILES + i)
+
+                x3_v[e_spare, i, :, lanes] = (
+                    p2_v[tile_rows(i), lanes] + dot(piece(2 * TILES + i)[...], b_v[e_slot, :n, lanes])
+                ).astype(x3_v.dtype)
+
+                @pl.when(i == 0)
+                def _():
+                    x3_half(TILES - 1, h).start()
+
+                @pl.when(i > 0)
+                def _():
+                    x2_half(i - 1, h).start()
+
+                return inner
+
+            lax.fori_loop(0, TILES, tile3, 0)
+            lax.fori_loop(0, TILES, tile2, 0)
+            x2_half(TILES - 1, h).start()
+            return carry
+
+        lax.fori_loop(0, 2, half_step, 0)
+        for s in range(2):
+            for i in range(TILES):
+                arrived(x3_v.at[s, i], x3_tx.at[s, i])
         l_exchange_drain()
         for s in range(5):
             arrived(own(lo), l3_tx.at[s])
@@ -310,9 +456,11 @@
                 pltpu.VMEM((2, rt, 3 * n), l_block.dtype),
                 pltpu.VMEM((2, TILES, rt, CHUNK), b_block.dtype),
                 pltpu.VMEM((2, rt, CHUNK), b_block.dtype),
-                dma((chunks,)), dma((chunks,)), dma((chunks,)), dma((3,)), dma((8,)), dma, dma,
+                pltpu.VMEM((n, CHUNK), jnp.float32),
+                pltpu.VMEM((n, CHUNK), jnp.float32),
+                dma((chunks + 1,)), dma((chunks,)), dma((chunks,)), dma((3,)), dma((8,)), dma, dma,
                 dma, dma, dma((3,)), dma((5,)), dma((2, TILES)),
-                dma((2, 4)), dma((2,)), dma((2,)), dma,
+                dma((2, 4)), dma((2,)), dma((2,)), dma, dma((12,)),
             ],
             compiler_params=pltpu.CompilerParams(has_side_effects=True, vmem_limit_bytes=66 * 1000 * 1000),
         )(l_block, b_block)

time: 774 us -> 762 us (0.984)
  Pallas kernels: 758 us -> 746 us
    pallas_call x1, Pallas kernels: 758 us -> 746 us  [local_product(): pl.pallas_call(kernel, out_shape=(jax.ShapeDtypeStruct((n, m), b_block.dt...]
where the time goes in v3:
time: 762 us; the launch traced here: 760 us
  Pallas kernels  746 us (98%)
  local copies, waits for them, and re-layouts  14.1 us (2%)
    pallas_call x1, Pallas kernels, local_product(): pl.pallas_call(kernel, out_shape=(jax.ShapeDtypeStruct((n, m), b_block.dt...  746 us

profile of v3, /device:TPU:24, one launch (start us, length us, event | category | flops | bytes accessed | tf_op | source)
XLA Modules:
  0.0 760.5 jit_solution(3251072441070683993)
XLA Ops:
  0.0 746.4 %shard_map.28 = (bf16[2048,4096]{1,0:T(8,128)(2,1)}, bf16[3,16,2048,256]{3,2,1,0:T(8,128)(2,1)}, bf16[2,4,2048,2048]{3,2,1,0:T(8,128)(2,1)}) custom-call(bf16[2048,2048]{1,0:T(8,128)(2,1)} %l_ref.1, bf16[2048,4096]{1,0:T(8,128)(2,1)} %b_ref.1), custom_call_target="tpu_custom_call" | custom-call | tf_op jit(solution)/shard_map/pallas_call | solution.py:444
  746.4 14.1 %copy.4 = bf16[2048,4096]{1,0:T(8,128)(2,1)} copy(bf16[2048,4096]{1,0:T(8,128)(2,1)} %get-tuple-element.6) | data formatting | bytes 33554432

commit v4 on v3

--- a/solution.py
+++ b/solution.py
@@ -8,6 +8,7 @@
 from jax.sharding import PartitionSpec as P
 
 MESH = pl.DeviceIdType.MESH
+PARTS = 8
 TILES = 4
 CHUNK = 256
 
@@ -27,7 +28,7 @@
 
 def kernel(
     l_ref, b_ref, x_ref, rb_ref, lg_ref,
-    l3_v, b_v, strip_v, x3_v, xo_v, p3_v, p2_v,
+    l3_v, b_v, strip_v, x3_v, xo_v, p3_v, p2_v, e0_v,
     b0_rx, b1_rx, b3_rx, l_rx, l3_rx, cross_rx, x3_rx,
     b_tx, fwd_tx, l_tx, l3_tx, x3_tx,
     load_sem, strip_sem, out_sem, l3_sem, piece_sem,
@@ -58,6 +59,21 @@
     def x_tile(i, c):
         return x_ref.at[pl.ds(pl.multiple_of(i * rt, rt), rt), pl.ds(pl.multiple_of(c * w, w), w)]
 
+    barrier = pltpu.get_barrier_semaphore()
+    greet = functools.partial(pl.semaphore_signal, barrier, inc=1, device_id_type=MESH)
+    greet(device_id=(batch, row, core_peer))
+    greet(device_id=(batch, row, y_peer))
+
+    @pl.when(row > 0)
+    def _():
+        greet(device_id=(batch, row - 1, col))
+
+    @pl.when(row < 3)
+    def _():
+        greet(device_id=(batch, row + 1, col))
+
+    pl.semaphore_wait(barrier, 4 - (row == 0).astype(jnp.int32) - (row == 3).astype(jnp.int32))
+
     def l_exchange_start():
         remote(l_ref, lg_ref.at[0, col], l_tx.at[0], l_rx.at[0], row, y_peer).start()
         remote(l_ref, lg_ref.at[0, col], l_tx.at[1], l_rx.at[1], row, core_peer).start()
@@ -178,8 +194,8 @@
                 remote(blk, blk, fwd_tx, b0_rx.at[c], 2, col).start()
                 continue
             for h in range(2):
-                part = blk.at[:, pl.ds(h * hw, hw)]
-                remote(part, part, fwd_tx, b0_rx.at[c + h], 2, col).start()
+                half_cols = pl.ds(h * hw, hw)
+                remote(blk.at[:, half_cols], e0_v.at[:, half_cols], fwd_tx, b0_rx.at[c + h], 2, col).start()
         l_forward()
         l_exchange_end()
         simple_rows(1, [(0, lambda c: rb_ref.at[0, c]), (1, own_chunk)])
@@ -329,16 +345,17 @@
         prefetch1(edge, e_slot)
         load1(edge, e_slot).wait()
 
-        def terms1(i, carry):
+        def terms1_x3(i, carry):
             rows = tile_rows(i)
             p3_v[rows, :] += dot(l3_v[rows, n : 2 * n], b_v[e_slot, n : 2 * n, :])
+            return carry
+
+        def terms1_x2(i, carry):
             piece_wait(TILES + i)
-            p2_v[rows, :] += dot(piece(TILES + i)[...], b_v[e_slot, n : 2 * n, :])
-            return carry
-
-        lax.fori_loop(0, TILES, terms1, 0)
-        for s in range(10, 12):
-            piece_start(s)
+            p2_v[tile_rows(i), :] += dot(piece(TILES + i)[...], b_v[e_slot, n : 2 * n, :])
+            return carry
+
+        lax.fori_loop(0, TILES, terms1_x3, 0)
         for s in range(2):
             for i in range(TILES):
                 x3_send(i, 0, s).wait_send()
@@ -346,31 +363,20 @@
         def half_lanes(h):
             return pl.ds(pl.multiple_of(h * hw, hw), hw)
 
-        def half_tile(i, h):
-            return x_ref.at[tile_rows(i), pl.ds(pl.multiple_of(edge * w + h * hw, hw), hw)]
-
         def x3_half(i, h):
+            lanes = pl.ds(pl.multiple_of(edge * w + h * hw, hw), hw)
             return remote(
-                x3_v.at[e_slot, i, :, half_lanes(h)], half_tile(i, h), x3_tx.at[e_slot, i], x3_rx, 3, col
-            )
-
-        def x2_half(i, h):
-            return pltpu.make_async_copy(
-                x3_v.at[e_spare, i, :, half_lanes(h)], half_tile(i, h), x3_tx.at[e_spare, i]
+                x3_v.at[e_slot, i, :, half_lanes(h)], x_ref.at[tile_rows(i), lanes], x3_tx.at[e_slot, i], x3_rx, 3, col
             )
 
         def half_step(h, carry):
             lanes = half_lanes(h)
-            part = rb_ref.at[0, edge, :, lanes]
-            arrived(part, b0_rx.at[edge + h])
-            last = pltpu.make_async_copy(part, b_v.at[e_slot, pl.ds(0, n), lanes], load_sem.at[e_slot, 0])
-            last.start()
-            last.wait()
-
-            def tile3(i, inner):
+            arrived(e0_v.at[:, lanes], b0_rx.at[edge + h])
+
+            def tile(i, inner):
                 rows = tile_rows(i)
                 x3_v[e_slot, i, :, lanes] = (
-                    p3_v[rows, lanes] + dot(l3_v[rows, :n], b_v[e_slot, :n, lanes])
+                    p3_v[rows, lanes] + dot(l3_v[rows, :n], e0_v[:, lanes])
                 ).astype(x3_v.dtype)
 
                 @pl.when(i > 0)
@@ -379,31 +385,36 @@
 
                 return inner
 
-            def tile2(i, inner):
-                @pl.when(h == 0)
-                def _():
-                    piece_wait(2 * TILES + i)
-
-                x3_v[e_spare, i, :, lanes] = (
-                    p2_v[tile_rows(i), lanes] + dot(piece(2 * TILES + i)[...], b_v[e_slot, :n, lanes])
-                ).astype(x3_v.dtype)
-
-                @pl.when(i == 0)
-                def _():
-                    x3_half(TILES - 1, h).start()
-
-                @pl.when(i > 0)
-                def _():
-                    x2_half(i - 1, h).start()
-
-                return inner
-
-            lax.fori_loop(0, TILES, tile3, 0)
-            lax.fori_loop(0, TILES, tile2, 0)
-            x2_half(TILES - 1, h).start()
+            lax.fori_loop(0, TILES, tile, 0)
+
+            @pl.when(h == 0)
+            def _():
+                lax.fori_loop(0, TILES, terms1_x2, 0)
+                for s in range(TILES + 6, 3 * TILES):
+                    piece_start(s)
+
+            x3_half(TILES - 1, h).start()
             return carry
 
         lax.fori_loop(0, 2, half_step, 0)
+
+        def x2_edge(i):
+            return pltpu.make_async_copy(x3_v.at[e_spare, i], x_tile(i, edge), x3_tx.at[e_spare, i])
+
+        def terms0_x2(i, carry):
+            piece_wait(2 * TILES + i)
+            x3_v[e_spare, i] = (
+                p2_v[tile_rows(i), :] + dot(piece(2 * TILES + i)[...], e0_v[...])
+            ).astype(x3_v.dtype)
+
+            @pl.when(i > 0)
+            def _():
+                x2_edge(i - 1).start()
+
+            return carry
+
+        lax.fori_loop(0, TILES, terms0_x2, 0)
+        x2_edge(TILES - 1).start()
         for s in range(2):
             for i in range(TILES):
                 arrived(x3_v.at[s, i], x3_tx.at[s, i])
@@ -430,6 +441,24 @@
             arrived(blk, l3_tx.at[s])
         arrived(b_ref, b_tx)
         arrived(x_ref, x3_rx)
+
+
+def copy_kernel(src_ref, dst_ref, buf, in_sem, out_sem):
+    parts, rows, _ = buf.shape
+
+    def fetch(s):
+        return pltpu.make_async_copy(src_ref.at[pl.ds(s * rows, rows)], buf.at[s], in_sem.at[s])
+
+    def store(s):
+        return pltpu.make_async_copy(buf.at[s], dst_ref.at[pl.ds(s * rows, rows)], out_sem.at[s])
+
+    for s in range(parts):
+        fetch(s).start()
+    for s in range(parts):
+        fetch(s).wait()
+        store(s).start()
+    for s in range(parts):
+        store(s).wait()
 
 
 def solution(mesh):
@@ -458,13 +487,21 @@
                 pltpu.VMEM((2, rt, CHUNK), b_block.dtype),
                 pltpu.VMEM((n, CHUNK), jnp.float32),
                 pltpu.VMEM((n, CHUNK), jnp.float32),
+                pltpu.VMEM((n, CHUNK), b_block.dtype),
                 dma((chunks + 1,)), dma((chunks,)), dma((chunks,)), dma((3,)), dma((8,)), dma, dma,
                 dma, dma, dma((3,)), dma((5,)), dma((2, TILES)),
                 dma((2, 4)), dma((2,)), dma((2,)), dma, dma((12,)),
             ],
-            compiler_params=pltpu.CompilerParams(has_side_effects=True, vmem_limit_bytes=66 * 1000 * 1000),
+            compiler_params=pltpu.CompilerParams(has_side_effects=True, collective_id=0, vmem_limit_bytes=66 * 1000 * 1000),
         )(l_block, b_block)
-        return x
+        return pl.pallas_call(
+            copy_kernel,
+            out_shape=jax.ShapeDtypeStruct((n, m), x.dtype),
+            in_specs=[hbm],
+            out_specs=hbm,
+            scratch_shapes=[pltpu.VMEM((PARTS, n // PARTS, m), x.dtype), dma((PARTS,)), dma((PARTS,))],
+            compiler_params=pltpu.CompilerParams(vmem_limit_bytes=66 * 1000 * 1000),
+        )(x)
 
     return jax.shard_map(
         local_product, mesh=mesh, in_specs=(block_spec, block_spec), out_specs=block_spec, check_vma=False

time: 762 us -> 749 us (0.983)
  local copies, waits for them, and re-layouts: 14.1 us -> 0 us
    unnamed x1 -> x0, local copies, waits for them, and re-layouts: 14.1 us -> none
    pallas_call x0 -> x1, Pallas kernels: none -> 11.8 us  [local_product(): pl.pallas_call(copy_kernel, out_shape=jax.ShapeDtypeStruct((n, m), x.dtyp...]
    pallas_call x1, Pallas kernels: 746 us -> 735 us  [local_product(): pl.pallas_call(kernel, out_shape=(jax.ShapeDtypeStruct((n, m), b_block.dt...]
where the time goes in v4:
time: 749 us; the launch traced here: 747 us
  Pallas kernels  747 us (100%)
    pallas_call x1, Pallas kernels, local_product(): pl.pallas_call(kernel, out_shape=(jax.ShapeDtypeStruct((n, m), b_block.dt...  735 us

profile of v4, /device:TPU:24, one launch (start us, length us, event | category | flops | bytes accessed | tf_op | source)
XLA Modules:
  0.0 747.2 jit_solution(16072751645964703016)
XLA Ops:
  0.0 735.4 %shard_map.28 = (bf16[2048,4096]{1,0:T(8,128)(2,1)}, bf16[3,16,2048,256]{3,2,1,0:T(8,128)(2,1)}, bf16[2,4,2048,2048]{3,2,1,0:T(8,128)(2,1)}) custom-call(bf16[2048,2048]{1,0:T(8,128)(2,1)} %l_ref.1, bf16[2048,4096]{1,0:T(8,128)(2,1)} %b_ref.1), custom_call_target="tpu_custom_call" | custom-call | tf_op jit(solution)/shard_map/pallas_call | solution.py:473
  735.4 11.8 %shard_map.29 = bf16[2048,4096]{1,0:T(8,128)(2,1)} custom-call(bf16[2048,4096]{1,0:T(8,128)(2,1)} %get-tuple-element.6.src_ref), custom_call_target="tpu_custom_call" | custom-call | tf_op jit(solution)/shard_map/pallas_call | solution.py:497

commit v5 on v2

--- a/solution.py
+++ b/solution.py
@@ -8,19 +8,30 @@
 from jax.sharding import PartitionSpec as P
 
 MESH = pl.DeviceIdType.MESH
+PARTS = 8
 TILES = 4
 CHUNK = 256
-
-
-def mid_order(chunks):
-    return [(1, c) for c in range(chunks)] + [(0, c) for c in range(chunks)]
+LAST = 2
+
+
+def mid_order(lead):
+    first = lead - 2
+    late = list(range(first, lead))
+    gap = -(-lead // 3)
+    order = [(1, c) for c in range(first)]
+    for c in range(lead):
+        order.append((0, c))
+        if late and (c + 1) % gap == 0:
+            order.append((1, late.pop(0)))
+    assert not late
+    return order
 
 
 def kernel(
     l_ref, b_ref, x_ref, rb_ref, lg_ref,
-    l3_v, b_v, strip_v, x3_v, xo_v,
-    b0_rx, b1_rx, b3_rx, l_rx, l3_rx, cross_rx, x3_rx,
-    b_tx, fwd_tx, l_tx, l3_tx, x3_tx,
+    l3_v, b_v, strip_v, x3_v, xo_v, xs_v,
+    b0_rx, b1_rx, b3_rx, l_rx, l2_rx, l3_rx, cross_rx, x3_rx, xs_rx,
+    b_tx, fwd_tx, l_tx, l2_tx, l3_tx, x3_tx, xs_tx,
     load_sem, strip_sem, out_sem, l3_sem,
 ):
     n, m = b_ref.shape
@@ -28,6 +39,7 @@
     rt = n // TILES
     w = CHUNK
     chunks = m // w
+    lead = chunks - LAST
     batch, row, col = (lax.axis_index(a) for a in ("batch", "row", "col"))
     core_peer = col + 1 - 2 * lax.rem(col, 2)
     y_peer = lax.rem(col + 2, 4)
@@ -42,11 +54,46 @@
     def arrived(dst, sem):
         pltpu.make_async_copy(dst, dst, sem).wait()
 
+    def lead_part(ref):
+        return ref.at[:, pl.ds(0, lead * w)]
+
+    def last_part(ref):
+        return ref.at[:, pl.ds(lead * w, LAST * w)]
+
+    def dot(a, b):
+        return jnp.dot(a, b, preferred_element_type=jnp.float32)
+
+    def tile_rows(i):
+        return pl.ds(pl.multiple_of(i * rt, rt), rt)
+
+    def l3_load():
+        for k in range(4):
+            pltpu.make_async_copy(lg_ref.at[1, k], l3_v.at[:, pl.ds(k * n, n)], l3_sem).start()
+
     def own_chunk(c):
         return b_ref.at[:, pl.ds(pl.multiple_of(c * w, w), w)]
 
     def x_tile(i, c):
         return x_ref.at[pl.ds(pl.multiple_of(i * rt, rt), rt), pl.ds(pl.multiple_of(c * w, w), w)]
+
+    barrier = pltpu.get_barrier_semaphore()
+    greet = functools.partial(pl.semaphore_signal, barrier, inc=1, device_id_type=MESH)
+    greet(device_id=(batch, row, core_peer))
+    greet(device_id=(batch, row, y_peer))
+
+    @pl.when(row > 0)
+    def _():
+        greet(device_id=(batch, row - 1, col))
+
+    @pl.when(row < 3)
+    def _():
+        greet(device_id=(batch, row + 1, col))
+
+    @pl.when((row == 1) | (row == 3))
+    def _():
+        greet(device_id=(batch, 4 - row, col))
+
+    pl.semaphore_wait(barrier, 3 + jnp.where(row == 0, 0, jnp.where(row == 1, 2, 1)))
 
     def l_exchange_start():
         remote(l_ref, lg_ref.at[0, col], l_tx.at[0], l_rx.at[0], row, y_peer).start()
@@ -87,14 +134,14 @@
     def load(c, slot, k, src):
         return pltpu.make_async_copy(src, b_v.at[slot, pl.ds(k * n, n), :], load_sem.at[slot, k])
 
-    def own_rows(r, c, slot):
+    def own_rows(r, c, slot, end):
         depth = (r + 1) * n
 
         def tile(i, carry):
             part = lax.rem(i, 2)
             strip_wait(r, i)
 
-            @pl.when((i + 1 < TILES) | (c + 1 < chunks))
+            @pl.when((i + 1 < TILES) | (c + 1 < end))
             def _():
                 strip_start(r, lax.rem(i + 1, TILES))
 
@@ -134,7 +181,7 @@
                 for cp in loads(c + 1, 1 - slot):
                     cp.start()
 
-            own_rows(r, c, slot)
+            own_rows(r, c, slot, chunks)
             return carry
 
         lax.fori_loop(0, chunks, step, 0)
@@ -158,24 +205,120 @@
     def _():
         l_exchange_start()
 
-        def send_own(c, carry):
-            remote(own_chunk(c), rb_ref.at[1, c], b_tx, b1_rx.at[c], 2, col).start()
+        def share(q, rx, tx):
+            own = lg_ref.at[q, col]
+            remote(own, own, tx.at[0], rx.at[1], row, y_peer).start()
+            remote(own, own, tx.at[1], rx.at[2], row, core_peer).start()
+
+        def share_forward(q, rx, tx):
+            blk = lg_ref.at[q, y_peer]
+            arrived(blk, rx.at[1])
+            remote(blk, blk, tx.at[2], rx.at[3], row, core_peer).start()
+
+        def share_end(q, rx):
+            arrived(lg_ref.at[q, core_peer], rx.at[2])
+            arrived(lg_ref.at[q, far], rx.at[3])
+
+        def b0_arrived(c):
+            arrived(rb_ref.at[0, c], b0_rx.at[c])
+
+        for k, c in mid_order(lead):
+            blk = rb_ref.at[k, c]
+            if k == 1:
+                remote(own_chunk(c), blk, b_tx, b1_rx.at[c], 2, col).start()
+                continue
+            b0_arrived(c)
+            remote(blk, blk, fwd_tx, b0_rx.at[c], 2, col).start()
+            if c == chunks // 2:
+                l_forward()
+                arrived(lg_ref.at[2, col], l2_rx.at[0])
+                share(2, l2_rx, l2_tx)
+        for c in range(lead, chunks):
+            b0_arrived(c)
+        arrived(lg_ref.at[1, col], l3_rx.at[0])
+        share(1, l3_rx, l3_tx)
+        share_forward(2, l2_rx, l2_tx)
+        share_end(2, l2_rx)
+
+        def last_loads(blocks):
+            return [load(lead + j, j, k, ref(lead + j)) for j in range(LAST) for k, ref in blocks]
+
+        b012 = [(0, lambda c: rb_ref.at[0, c]), (1, own_chunk), (2, lambda c: rb_ref.at[1, c])]
+        b3 = [(3, lambda c: rb_ref.at[2, c])]
+
+        def send_last(q, r):
+            def one(t, carry):
+                i, j = t // LAST, lax.rem(t, LAST)
+                remote(xs_v.at[q, j, i], x_tile(i, lead + j), xs_tx.at[q], xs_rx.at[q], r, col).start()
+                return carry
+
+            lax.fori_loop(0, TILES * LAST, one, 0)
+
+        for c in range(lead, chunks):
+            arrived(rb_ref.at[1, c], b1_rx.at[c])
+        for cp in last_loads(b012):
+            cp.start()
+
+        def last_strip(i):
+            part = lax.rem(i, 2)
+            return [
+                pltpu.make_async_copy(
+                    lg_ref.at[2, k, tile_rows(i)], strip_v.at[part, :, pl.ds(k * n, n)], strip_sem.at[part]
+                )
+                for k in range(3)
+            ]
+
+        for cp in last_strip(0):
+            cp.start()
+        for cp in last_loads(b012):
+            cp.wait()
+
+        def tile2(i, carry):
+            for cp in last_strip(i):
+                cp.wait()
+
+            @pl.when(i + 1 < TILES)
+            def _():
+                for cp in last_strip(i + 1):
+                    cp.start()
+
+            for j in range(LAST):
+                xs_v[0, j, i] = dot(strip_v[lax.rem(i, 2)], b_v[j, : 3 * n, :]).astype(xs_v.dtype)
             return carry
 
-        def forward(c, carry):
-            blk = rb_ref.at[0, c]
-            arrived(blk, b0_rx.at[c])
-            remote(blk, blk, fwd_tx, b0_rx.at[c], 2, col).start()
-            return carry
-
-        lax.fori_loop(0, chunks, send_own, 0)
-        lax.fori_loop(0, chunks, forward, 0)
-        l_forward()
+        lax.fori_loop(0, TILES, tile2, 0)
+        send_last(0, 2)
+
         l_exchange_end()
         simple_rows(1, [(0, lambda c: rb_ref.at[0, c]), (1, own_chunk)])
+
+        share_forward(1, l3_rx, l3_tx)
+        share_end(1, l3_rx)
+        l3_load()
+        for c in range(lead, chunks):
+            arrived(rb_ref.at[2, c], b3_rx.at[c])
+        for cp in last_loads(b012 + b3):
+            cp.start()
+        for cp in last_loads(b012 + b3):
+            cp.wait()
+        arrived(l3_v, l3_sem)
+
+        def tile3(i, carry):
+            for j in range(LAST):
+                xs_v[1, j, i] = dot(l3_v[tile_rows(i), :], b_v[j]).astype(xs_v.dtype)
+            return carry
+
+        lax.fori_loop(0, TILES, tile3, 0)
+        send_last(1, 3)
+
         l_exchange_drain()
-        arrived(b_ref, b_tx)
-        arrived(rb_ref.at[0], fwd_tx)
+        for s in range(3):
+            arrived(l_ref, l2_tx.at[s])
+            arrived(l_ref, l3_tx.at[s])
+        arrived(lead_part(b_ref), b_tx)
+        arrived(lead_part(b_ref), fwd_tx)
+        for q in range(2):
+            arrived(xs_v.at[q], xs_tx.at[q])
 
     @pl.when(row == 2)
     def _():
@@ -187,11 +330,16 @@
 
         def other(p):
             return lg_ref.at[1, y_peer, p]
+
+        remote(l_ref, lg_ref.at[2, col], l2_tx.at[0], l2_rx.at[0], 1, col).start()
+        for c in range(lead, chunks):
+            remote(own_chunk(c), rb_ref.at[1, c], b_tx, b1_rx.at[c], 1, col).start()
 
         arrived(own(lo), l3_rx.at[0])
         remote(own(lo), own(lo), l3_tx.at[0], l3_rx.at[2], row, y_peer).start()
         remote(own(lo), own(lo), l3_tx.at[1], l3_rx.at[4], row, core_peer).start()
         arrived(own(hi), l3_rx.at[1])
+        remote(lg_ref.at[1, col], lg_ref.at[1, col], l2_tx.at[1], l3_rx.at[0], 1, col).start()
         remote(own(hi), own(hi), l3_tx.at[2], l3_rx.at[5], row, core_peer).start()
         l_forward()
         arrived(other(lo), l3_rx.at[2])
@@ -201,13 +349,12 @@
         l_exchange_end()
         for s, (blk, p) in enumerate(((core_peer, lo), (core_peer, hi), (far, lo), (far, hi))):
             arrived(lg_ref.at[1, blk, p], l3_rx.at[4 + s])
-        for k in range(4):
-            pltpu.make_async_copy(lg_ref.at[1, k], l3_v.at[:, pl.ds(k * n, n)], l3_sem).start()
+        l3_load()
 
         def early(c, slot):
-            return [
+            return (
                 load(c, slot, 1, rb_ref.at[1, c]), load(c, slot, 2, own_chunk(c)), load(c, slot, 3, rb_ref.at[2, c])
-            ]
+            )
 
         def prefetch(c, slot):
             arrived(rb_ref.at[1, c], b1_rx.at[c])
@@ -227,9 +374,8 @@
             arrived(rb_ref.at[0, c], b0_rx.at[c])
             last = load(c, slot, 0, rb_ref.at[0, c])
             last.start()
-            for cp in early(c, slot):
+            for cp in (*early(c, slot), last):
                 cp.wait()
-            last.wait()
             def tile(i, inner):
                 @pl.when(c >= 2)
                 def _():
@@ -248,19 +394,24 @@
 
             lax.fori_loop(0, TILES, tile, 0)
 
-            @pl.when(c + 1 < chunks)
+            x3_send(TILES - 1, c, slot).start()
+
+            @pl.when(c + 1 < lead)
             def _():
                 prefetch(c + 1, 1 - slot)
 
-            x3_send(TILES - 1, c, slot).start()
-            own_rows(2, c, slot)
+            own_rows(2, c, slot, lead)
             return carry
 
-        lax.fori_loop(0, chunks, step, 0)
+        lax.fori_loop(0, lead, step, 0)
         own_rows_drain()
-        for slot in range(2):
+        for s in range(2):
             for i in range(TILES):
-                x3_send(i, 0, slot).wait_send()
+                x3_send(i, 0, s).wait_send()
+        arrived(last_part(x_ref), xs_rx.at[0])
+        for s in range(2):
+            arrived(l_ref, l2_tx.at[s])
+        arrived(last_part(b_ref), b_tx)
         l_exchange_drain()
         for s in range(5):
             arrived(own(lo), l3_tx.at[s])
@@ -275,15 +426,40 @@
         arrived(blk, cross_rx)
         remote(blk, blk, l3_tx.at[3], l3_rx.at[3], 2, col).start()
 
-        def send(c, carry):
-            remote(own_chunk(c), rb_ref.at[2, c], b_tx, b3_rx.at[c], 2, col).start()
-            return carry
-
-        lax.fori_loop(0, chunks, send, 0)
+        def send(first, end, r):
+            def one(c, carry):
+                remote(own_chunk(c), rb_ref.at[2, c], b_tx, b3_rx.at[c], r, col).start()
+                return carry
+
+            lax.fori_loop(first, end, one, 0)
+
+        mark = lead * 5 // 7
+        send(0, mark, 2)
+        send(lead, chunks, 1)
+        send(mark, lead, 2)
         for s in range(4):
             arrived(blk, l3_tx.at[s])
         arrived(b_ref, b_tx)
-        arrived(x_ref, x3_rx)
+        arrived(lead_part(x_ref), x3_rx)
+        arrived(last_part(x_ref), xs_rx.at[1])
+
+
+def copy_kernel(src_ref, dst_ref, buf, in_sem, out_sem):
+    parts, rows, _ = buf.shape
+
+    def fetch(s):
+        return pltpu.make_async_copy(src_ref.at[pl.ds(s * rows, rows)], buf.at[s], in_sem.at[s])
+
+    def store(s):
+        return pltpu.make_async_copy(buf.at[s], dst_ref.at[pl.ds(s * rows, rows)], out_sem.at[s])
+
+    for s in range(parts):
+        fetch(s).start()
+    for s in range(parts):
+        fetch(s).wait()
+        store(s).start()
+    for s in range(parts):
+        store(s).wait()
 
 
 def solution(mesh):
@@ -300,7 +476,7 @@
             out_shape=(
                 jax.ShapeDtypeStruct((n, m), b_block.dtype),
                 jax.ShapeDtypeStruct((3, chunks, n, CHUNK), b_block.dtype),
-                jax.ShapeDtypeStruct((2, 4, n, n), l_block.dtype),
+                jax.ShapeDtypeStruct((3, 4, n, n), l_block.dtype),
             ),
             in_specs=[hbm, hbm],
             out_specs=(hbm, hbm, hbm),
@@ -310,13 +486,21 @@
                 pltpu.VMEM((2, rt, 3 * n), l_block.dtype),
                 pltpu.VMEM((2, TILES, rt, CHUNK), b_block.dtype),
                 pltpu.VMEM((2, rt, CHUNK), b_block.dtype),
-                dma((chunks,)), dma((chunks,)), dma((chunks,)), dma((3,)), dma((8,)), dma, dma,
-                dma, dma, dma((3,)), dma((5,)), dma((2, TILES)),
+                pltpu.VMEM((2, LAST, TILES, rt, CHUNK), b_block.dtype),
+                dma((chunks,)), dma((chunks,)), dma((chunks,)), dma((3,)), dma((4,)), dma((8,)), dma, dma, dma((2,)),
+                dma, dma, dma((3,)), dma((3,)), dma((5,)), dma((2, TILES)), dma((2,)),
                 dma((2, 4)), dma((2,)), dma((2,)), dma,
             ],
-            compiler_params=pltpu.CompilerParams(has_side_effects=True, vmem_limit_bytes=66 * 1000 * 1000),
+            compiler_params=pltpu.CompilerParams(has_side_effects=True, collective_id=0, vmem_limit_bytes=66 * 1000 * 1000),
         )(l_block, b_block)
-        return x
+        return pl.pallas_call(
+            copy_kernel,
+            out_shape=jax.ShapeDtypeStruct((n, m), x.dtype),
+            in_specs=[hbm],
+            out_specs=hbm,
+            scratch_shapes=[pltpu.VMEM((PARTS, n // PARTS, m), x.dtype), dma((PARTS,)), dma((PARTS,))],
+            compiler_params=pltpu.CompilerParams(vmem_limit_bytes=66 * 1000 * 1000),
+        )(x)
 
     return jax.shard_map(
         local_product, mesh=mesh, in_specs=(block_spec, block_spec), out_specs=block_spec, check_vma=False

time: 774 us -> 737 us (0.952)
  Pallas kernels: 758 us -> 735 us
  local copies, waits for them, and re-layouts: 14.1 us -> 0 us
    pallas_call x1, Pallas kernels: 758 us -> 724 us  [local_product(): pl.pallas_call(kernel, out_shape=(jax.ShapeDtypeStruct((n, m), b_block.dt...]
    unnamed x1 -> x0, local copies, waits for them, and re-layouts: 14.1 us -> none
    pallas_call x0 -> x1, Pallas kernels: none -> 11.8 us  [local_product(): pl.pallas_call(copy_kernel, out_shape=jax.ShapeDtypeStruct((n, m), x.dtyp...]
where the time goes in v5:
time: 737 us; the launch traced here: 735 us
  Pallas kernels  735 us (100%)
    pallas_call x1, Pallas kernels, local_product(): pl.pallas_call(kernel, out_shape=(jax.ShapeDtypeStruct((n, m), b_block.dt...  724 us

profile of v5, /device:TPU:24, one launch (start us, length us, event | category | flops | bytes accessed | tf_op | source)
XLA Modules:
  0.0 735.3 jit_solution(4218250991524350622)
XLA Ops:
  0.0 723.5 %shard_map.28 = (bf16[2048,4096]{1,0:T(8,128)(2,1)}, bf16[3,16,2048,256]{3,2,1,0:T(8,128)(2,1)}, bf16[3,4,2048,2048]{3,2,1,0:T(8,128)(2,1)}) custom-call(bf16[2048,2048]{1,0:T(8,128)(2,1)} %l_ref.1, bf16[2048,4096]{1,0:T(8,128)(2,1)} %b_ref.1), custom_call_target="tpu_custom_call" | custom-call | tf_op jit(solution)/shard_map/pallas_call | solution.py:474
  723.5 11.8 %shard_map.29 = bf16[2048,4096]{1,0:T(8,128)(2,1)} custom-call(bf16[2048,4096]{1,0:T(8,128)(2,1)} %get-tuple-element.6.src_ref), custom_call_target="tpu_custom_call" | custom-call | tf_op jit(solution)/shard_map/pallas_call | solution.py:496

commit v6 on v5

--- a/solution.py
+++ b/solution.py
@@ -11,6 +11,7 @@
 PARTS = 8
 TILES = 4
 CHUNK = 256
+TAIL = 256
 LAST = 2
 
 
@@ -28,7 +29,7 @@
 
 
 def kernel(
-    l_ref, b_ref, x_ref, rb_ref, lg_ref,
+    l_ref, b_ref, x_ref, rb_ref, lg_ref, t_ref,
     l3_v, b_v, strip_v, x3_v, xo_v, xs_v,
     b0_rx, b1_rx, b3_rx, l_rx, l2_rx, l3_rx, cross_rx, x3_rx, xs_rx,
     b_tx, fwd_tx, l_tx, l2_tx, l3_tx, x3_tx, xs_tx,
@@ -248,11 +249,11 @@
 
         def send_last(q, r):
             def one(t, carry):
-                i, j = t // LAST, lax.rem(t, LAST)
+                i, j = lax.rem(t, TILES), t // TILES
                 remote(xs_v.at[q, j, i], x_tile(i, lead + j), xs_tx.at[q], xs_rx.at[q], r, col).start()
                 return carry
 
-            lax.fori_loop(0, TILES * LAST, one, 0)
+            lax.fori_loop(0, TILES * LAST if q == 0 else TILES * (LAST - 1), one, 0)
 
         for c in range(lead, chunks):
             arrived(rb_ref.at[1, c], b1_rx.at[c])
@@ -310,6 +311,8 @@
 
         lax.fori_loop(0, TILES, tile3, 0)
         send_last(1, 3)
+        for i in range(TILES):
+            pltpu.make_async_copy(xs_v.at[1, LAST - 1, i], t_ref.at[pl.ds(i * rt, rt)], xs_tx.at[2]).start()
 
         l_exchange_drain()
         for s in range(3):
@@ -317,8 +320,9 @@
             arrived(l_ref, l3_tx.at[s])
         arrived(lead_part(b_ref), b_tx)
         arrived(lead_part(b_ref), fwd_tx)
-        for q in range(2):
-            arrived(xs_v.at[q], xs_tx.at[q])
+        arrived(xs_v.at[0], xs_tx.at[0])
+        arrived(xs_v.at[1, pl.ds(0, LAST - 1)], xs_tx.at[1])
+        arrived(t_ref, xs_tx.at[2])
 
     @pl.when(row == 2)
     def _():
@@ -441,7 +445,7 @@
             arrived(blk, l3_tx.at[s])
         arrived(b_ref, b_tx)
         arrived(lead_part(x_ref), x3_rx)
-        arrived(last_part(x_ref), xs_rx.at[1])
+        arrived(x_ref.at[:, pl.ds(lead * w, LAST * w - TAIL)], xs_rx.at[1])
 
 
 def copy_kernel(src_ref, dst_ref, buf, in_sem, out_sem):
@@ -462,6 +466,16 @@
         store(s).wait()
 
 
+def tail_kernel(x_ref, tail_ref, out_ref, sem):
+    del x_ref
+
+    @pl.when(lax.axis_index("row") == 3)
+    def _():
+        store = pltpu.make_async_copy(tail_ref, out_ref.at[:, pl.ds(out_ref.shape[1] - TAIL, TAIL)], sem)
+        store.start()
+        store.wait()
+
+
 def solution(mesh):
     block_spec = P(("batch", "row"), "col")
 
@@ -471,15 +485,16 @@
         chunks = m // CHUNK
         dma = pltpu.SemaphoreType.DMA
         hbm = pl.BlockSpec(memory_space=pl.ANY)
-        x, _, _ = pl.pallas_call(
+        x, _, _, tail = pl.pallas_call(
             kernel,
             out_shape=(
                 jax.ShapeDtypeStruct((n, m), b_block.dtype),
                 jax.ShapeDtypeStruct((3, chunks, n, CHUNK), b_block.dtype),
                 jax.ShapeDtypeStruct((3, 4, n, n), l_block.dtype),
+                jax.ShapeDtypeStruct((n, TAIL), b_block.dtype),
             ),
             in_specs=[hbm, hbm],
-            out_specs=(hbm, hbm, hbm),
+            out_specs=(hbm, hbm, hbm, hbm),
             scratch_shapes=[
                 pltpu.VMEM((n, 4 * n), l_block.dtype),
                 pltpu.VMEM((2, 4 * n, CHUNK), b_block.dtype),
@@ -488,19 +503,29 @@
                 pltpu.VMEM((2, rt, CHUNK), b_block.dtype),
                 pltpu.VMEM((2, LAST, TILES, rt, CHUNK), b_block.dtype),
                 dma((chunks,)), dma((chunks,)), dma((chunks,)), dma((3,)), dma((4,)), dma((8,)), dma, dma, dma((2,)),
-                dma, dma, dma((3,)), dma((3,)), dma((5,)), dma((2, TILES)), dma((2,)),
+                dma, dma, dma((3,)), dma((3,)), dma((5,)), dma((2, TILES)), dma((3,)),
                 dma((2, 4)), dma((2,)), dma((2,)), dma,
             ],
             compiler_params=pltpu.CompilerParams(has_side_effects=True, collective_id=0, vmem_limit_bytes=66 * 1000 * 1000),
         )(l_block, b_block)
-        return pl.pallas_call(
+        tail = lax.ppermute(tail, "row", [(1, 3)])
+        x = pl.pallas_call(
             copy_kernel,
             out_shape=jax.ShapeDtypeStruct((n, m), x.dtype),
             in_specs=[hbm],
             out_specs=hbm,
             scratch_shapes=[pltpu.VMEM((PARTS, n // PARTS, m), x.dtype), dma((PARTS,)), dma((PARTS,))],
             compiler_params=pltpu.CompilerParams(vmem_limit_bytes=66 * 1000 * 1000),
+            cost_estimate=pl.CostEstimate(flops=4 * 10**9, bytes_accessed=4 * n * m, transcendentals=0),
         )(x)
+        return pl.pallas_call(
+            tail_kernel,
+            out_shape=jax.ShapeDtypeStruct((n, m), x.dtype),
+            in_specs=[hbm, pl.BlockSpec(memory_space=pltpu.VMEM)],
+            out_specs=hbm,
+            input_output_aliases={0: 0},
+            scratch_shapes=[dma],
+        )(x, tail)
 
     return jax.shard_map(
         local_product, mesh=mesh, in_specs=(block_spec, block_spec), out_specs=block_spec, check_vma=False

time: 737 us -> 732 us (level)
  Pallas kernels: 735 us -> 715 us
  waiting for transfers between devices: 0 us -> 13.9 us
    pallas_call x1, Pallas kernels: 724 us -> 701 us  [local_product(): pl.pallas_call(kernel, out_shape=(jax.ShapeDtypeStruct((n, m), b_block.dt...]
    ppermute x0 -> x1, waiting for transfers between devices: none -> 13.9 us  [local_product(): tail = lax.ppermute(tail, 'row', [(1, 3)])]
  transfers between devices with their start and end apart: 0 -> 1, of which waited for: 0 -> 1; matrix products, arithmetic and copies ran while one was open for 0% -> 0% of each run, Pallas kernels for 0% -> 2%
where the time goes in v6:
time: 732 us; the launch traced here: 730 us
  Pallas kernels  715 us (98%)
  waiting for transfers between devices  13.9 us (2%)
    pallas_call x1, Pallas kernels, local_product(): pl.pallas_call(kernel, out_shape=(jax.ShapeDtypeStruct((n, m), b_block.dt...  701 us
  transfers between devices with their start and end apart: 1, of which 1 were waited for; matrix products, arithmetic and copies ran while one was open for 0% of the time, Pallas kernels for 2%

profile of v6, /device:TPU:24, one launch (start us, length us, event | category | flops | bytes accessed | tf_op | source)
XLA Modules:
  0.0 730.3 jit_solution(8952162888974063294)
XLA Ops:
  0.0 701.1 %shard_map.28 = (bf16[2048,4096]{1,0:T(8,128)(2,1)}, bf16[3,16,2048,256]{3,2,1,0:T(8,128)(2,1)}, bf16[3,4,2048,2048]{3,2,1,0:T(8,128)(2,1)}, bf16[2048,256]{1,0:T(8,128)(2,1)}) custom-call(bf16[2048,2048]{1,0:T(8,128)(2,1)} %l_ref.1, bf16[2048,4096]{1,0:T(8,128)(2,1)} %b_ref.1), custom_call_target="tpu_custom_call" | custom-call | tf_op jit(solution)/shard_map/pallas_call | solution.py:488
  701.1 1.3 collective-permute-start
  702.4 11.8 %shard_map.29.x_ref = bf16[2048,4096]{1,0:T(8,128)(2,1)} custom-call(bf16[2048,4096]{1,0:T(8,128)(2,1)} %get-tuple-element.7.src_ref), custom_call_target="tpu_custom_call" | custom-call | flops 4000000000 | bytes 33554432 | tf_op jit(solution)/shard_map/pallas_call | solution.py:512
  714.2 13.9 %collective-permute-done.tail_ref = bf16[2048,256]{1,0:T(8,128)(2,1)} collective-permute-done((bf16[2048,256]{1,0:T(8,128)(2,1)}, bf16[2048,256]{1,0:T(8,128)(2,1)}, u32[]{:S(2)}, u32[]{:S(2)}) %collective-permute-start) | collective-permute-done | bytes 1048608 | tf_op jit(solution)/shard_map/ppermute | solution.py:511
  728.1 2.2 shard_map.30
Async XLA Ops:
  701.1 27.0 %collective-permute-start = (bf16[2048,256]{1,0:T(8,128)(2,1)}, bf16[2048,256]{1,0:T(8,128)(2,1)}, u32[]{:S(2)}, u32[]{:S(2)}) collective-permute-start(bf16[2048,256]{1,0:T(8,128)(2,1)} %get-tuple-element.8), channel_id=1, source_target_pairs={{4,12},{5,13},{6,14},{7,15},{20,28},{21,29},{22,30},{23,31}} | collective-permute-start | bytes 3145736 | tf_op jit(solution)/shard_map/ppermute | solution.py:511

commit v7 on v6

--- a/solution.py
+++ b/solution.py
@@ -247,13 +247,12 @@
         b012 = [(0, lambda c: rb_ref.at[0, c]), (1, own_chunk), (2, lambda c: rb_ref.at[1, c])]
         b3 = [(3, lambda c: rb_ref.at[2, c])]
 
-        def send_last(q, r):
-            def one(t, carry):
-                i, j = lax.rem(t, TILES), t // TILES
+        def send_last(q, r, j):
+            def one(i, carry):
                 remote(xs_v.at[q, j, i], x_tile(i, lead + j), xs_tx.at[q], xs_rx.at[q], r, col).start()
                 return carry
 
-            lax.fori_loop(0, TILES * LAST if q == 0 else TILES * (LAST - 1), one, 0)
+            lax.fori_loop(0, TILES, one, 0)
 
         for c in range(lead, chunks):
             arrived(rb_ref.at[1, c], b1_rx.at[c])
@@ -288,7 +287,7 @@
             return carry
 
         lax.fori_loop(0, TILES, tile2, 0)
-        send_last(0, 2)
+        send_last(0, 2, 0)
 
         l_exchange_end()
         simple_rows(1, [(0, lambda c: rb_ref.at[0, c]), (1, own_chunk)])
@@ -310,7 +309,10 @@
             return carry
 
         lax.fori_loop(0, TILES, tile3, 0)
-        send_last(1, 3)
+        for j in range(LAST - 1):
+            send_last(1, 3, j)
+        for j in range(1, LAST):
+            send_last(0, 2, j)
         for i in range(TILES):
             pltpu.make_async_copy(xs_v.at[1, LAST - 1, i], t_ref.at[pl.ds(i * rt, rt)], xs_tx.at[2]).start()
 

time: 732 us -> 728 us (level)
  no operation moved by 1% of the time
where the time goes in v7:
time: 728 us; the launch traced here: 726 us
  Pallas kernels  711 us (98%)
  waiting for transfers between devices  14.1 us (2%)
    pallas_call x1, Pallas kernels, local_product(): pl.pallas_call(kernel, out_shape=(jax.ShapeDtypeStruct((n, m), b_block.dt...  697 us
  transfers between devices with their start and end apart: 1, of which 1 were waited for; matrix products, arithmetic and copies ran while one was open for 0% of the time, Pallas kernels for 2%

profile of v7, /device:TPU:24, one launch (start us, length us, event | category | flops | bytes accessed | tf_op | source)
XLA Modules:
  0.0 726.5 jit_solution(11486514720635084368)
XLA Ops:
  0.0 697.0 %shard_map.28 = (bf16[2048,4096]{1,0:T(8,128)(2,1)}, bf16[3,16,2048,256]{3,2,1,0:T(8,128)(2,1)}, bf16[3,4,2048,2048]{3,2,1,0:T(8,128)(2,1)}, bf16[2048,256]{1,0:T(8,128)(2,1)}) custom-call(bf16[2048,2048]{1,0:T(8,128)(2,1)} %l_ref.1, bf16[2048,4096]{1,0:T(8,128)(2,1)} %b_ref.1), custom_call_target="tpu_custom_call" | custom-call | tf_op jit(solution)/shard_map/pallas_call | solution.py:490
  697.1 1.3 collective-permute-start
  698.4 11.8 %shard_map.29.x_ref = bf16[2048,4096]{1,0:T(8,128)(2,1)} custom-call(bf16[2048,4096]{1,0:T(8,128)(2,1)} %get-tuple-element.7.src_ref), custom_call_target="tpu_custom_call" | custom-call | flops 4000000000 | bytes 33554432 | tf_op jit(solution)/shard_map/pallas_call | solution.py:514
  710.2 14.1 %collective-permute-done.tail_ref = bf16[2048,256]{1,0:T(8,128)(2,1)} collective-permute-done((bf16[2048,256]{1,0:T(8,128)(2,1)}, bf16[2048,256]{1,0:T(8,128)(2,1)}, u32[]{:S(2)}, u32[]{:S(2)}) %collective-permute-start) | collective-permute-done | bytes 1048608 | tf_op jit(solution)/shard_map/ppermute | solution.py:513
  724.3 2.2 shard_map.30
Async XLA Ops:
  697.1 27.2 %collective-permute-start = (bf16[2048,256]{1,0:T(8,128)(2,1)}, bf16[2048,256]{1,0:T(8,128)(2,1)}, u32[]{:S(2)}, u32[]{:S(2)}) collective-permute-start(bf16[2048,256]{1,0:T(8,128)(2,1)} %get-tuple-element.8), channel_id=1, source_target_pairs={{4,12},{5,13},{6,14},{7,15},{20,28},{21,29},{22,30},{23,31}} | collective-permute-start | bytes 3145736 | tf_op jit(solution)/shard_map/ppermute | solution.py:513

commit v8 on v7

--- a/solution.py
+++ b/solution.py
@@ -309,12 +309,10 @@
             return carry
 
         lax.fori_loop(0, TILES, tile3, 0)
-        for j in range(LAST - 1):
+        for j in range(LAST):
             send_last(1, 3, j)
-        for j in range(1, LAST):
-            send_last(0, 2, j)
         for i in range(TILES):
-            pltpu.make_async_copy(xs_v.at[1, LAST - 1, i], t_ref.at[pl.ds(i * rt, rt)], xs_tx.at[2]).start()
+            pltpu.make_async_copy(xs_v.at[0, LAST - 1, i], t_ref.at[pl.ds(i * rt, rt)], xs_tx.at[2]).start()
 
         l_exchange_drain()
         for s in range(3):
@@ -322,8 +320,8 @@
             arrived(l_ref, l3_tx.at[s])
         arrived(lead_part(b_ref), b_tx)
         arrived(lead_part(b_ref), fwd_tx)
-        arrived(xs_v.at[0], xs_tx.at[0])
-        arrived(xs_v.at[1, pl.ds(0, LAST - 1)], xs_tx.at[1])
+        arrived(xs_v.at[0, pl.ds(0, LAST - 1)], xs_tx.at[0])
+        arrived(xs_v.at[1], xs_tx.at[1])
         arrived(t_ref, xs_tx.at[2])
 
     @pl.when(row == 2)
@@ -414,7 +412,7 @@
         for s in range(2):
             for i in range(TILES):
                 x3_send(i, 0, s).wait_send()
-        arrived(last_part(x_ref), xs_rx.at[0])
+        arrived(x_ref.at[:, pl.ds(lead * w, LAST * w - TAIL)], xs_rx.at[0])
         for s in range(2):
             arrived(l_ref, l2_tx.at[s])
         arrived(last_part(b_ref), b_tx)
@@ -447,7 +445,7 @@
             arrived(blk, l3_tx.at[s])
         arrived(b_ref, b_tx)
         arrived(lead_part(x_ref), x3_rx)
-        arrived(x_ref.at[:, pl.ds(lead * w, LAST * w - TAIL)], xs_rx.at[1])
+        arrived(last_part(x_ref), xs_rx.at[1])
 
 
 def copy_kernel(src_ref, dst_ref, buf, in_sem, out_sem):
@@ -471,7 +469,7 @@
 def tail_kernel(x_ref, tail_ref, out_ref, sem):
     del x_ref
 
-    @pl.when(lax.axis_index("row") == 3)
+    @pl.when(lax.axis_index("row") == 2)
     def _():
         store = pltpu.make_async_copy(tail_ref, out_ref.at[:, pl.ds(out_ref.shape[1] - TAIL, TAIL)], sem)
         store.start()
@@ -510,7 +508,7 @@
             ],
             compiler_params=pltpu.CompilerParams(has_side_effects=True, collective_id=0, vmem_limit_bytes=66 * 1000 * 1000),
         )(l_block, b_block)
-        tail = lax.ppermute(tail, "row", [(1, 3)])
+        tail = lax.ppermute(tail, "row", [(1, 2)])
         x = pl.pallas_call(
             copy_kernel,
             out_shape=jax.ShapeDtypeStruct((n, m), x.dtype),

time: 728 us -> 748 us (1.027); the launches traced: 726 us -> 734 us
  Pallas kernels: 711 us -> 733 us
  waiting for transfers between devices: 14.1 us -> 0.01 us
    pallas_call x1, Pallas kernels: 697 us -> 720 us  [local_product(): pl.pallas_call(kernel, out_shape=(jax.ShapeDtypeStruct((n, m), b_block.dt...]
    ppermute x1, waiting for transfers between devices: 14.1 us -> 0.01 us  [local_product(): tail = lax.ppermute(tail, 'row', [(1, 2)])]
  transfers between devices with their start and end apart: 1 -> 1, of which waited for: 1 -> 0; matrix products, arithmetic and copies ran while one was open for 0% -> 0% of each run, Pallas kernels for 2% -> 2%
where the time goes in v8:
time: 748 us; the launch traced here: 734 us
  Pallas kernels  733 us (98%)
    pallas_call x1, Pallas kernels, local_product(): pl.pallas_call(kernel, out_shape=(jax.ShapeDtypeStruct((n, m), b_block.dt...  720 us
  transfers between devices with their start and end apart: 1, of which 0 were waited for; matrix products, arithmetic and copies ran while one was open for 0% of the time, Pallas kernels for 2%

profile of v8, /device:TPU:24, one launch (start us, length us, event | category | flops | bytes accessed | tf_op | source)
XLA Modules:
  0.0 734.3 jit_solution(3322642703066554708)
XLA Ops:
  0.0 719.6 %shard_map.28 = (bf16[2048,4096]{1,0:T(8,128)(2,1)}, bf16[3,16,2048,256]{3,2,1,0:T(8,128)(2,1)}, bf16[3,4,2048,2048]{3,2,1,0:T(8,128)(2,1)}, bf16[2048,256]{1,0:T(8,128)(2,1)}) custom-call(bf16[2048,2048]{1,0:T(8,128)(2,1)} %l_ref.1, bf16[2048,4096]{1,0:T(8,128)(2,1)} %b_ref.1), custom_call_target="tpu_custom_call" | custom-call | tf_op jit(solution)/shard_map/pallas_call | solution.py:488
  719.6 1.6 collective-permute-start
  721.2 11.8 %shard_map.29.x_ref = bf16[2048,4096]{1,0:T(8,128)(2,1)} custom-call(bf16[2048,4096]{1,0:T(8,128)(2,1)} %get-tuple-element.7.src_ref), custom_call_target="tpu_custom_call" | custom-call | flops 4000000000 | bytes 33554432 | tf_op jit(solution)/shard_map/pallas_call | solution.py:512
  733.0 0.0 collective-permute-done.tail_ref
  733.0 1.2 shard_map.30
Async XLA Ops:
  719.6 13.5 %collective-permute-start = (bf16[2048,256]{1,0:T(8,128)(2,1)}, bf16[2048,256]{1,0:T(8,128)(2,1)}, u32[]{:S(2)}, u32[]{:S(2)}) collective-permute-start(bf16[2048,256]{1,0:T(8,128)(2,1)} %get-tuple-element.8), channel_id=1, source_target_pairs={{4,8},{5,9},{6,10},{7,11},{20,24},{21,25},{22,26},{23,27}} | collective-permute-start | bytes 3145736 | tf_op jit(solution)/shard_map/ppermute | solution.py:511
